TPU v7x, 512 devices: a whole 4x8x8 slice. The times are simulated.
512 devices in a mesh: gy: 64 (over z, y_lo, core), gz: 8 (over y_hi, x).
Axes of the slice: x: 4, y: 8 (y_hi: 2, y_lo: 4; y = y_hi * 4 + y_lo), z: 8, core: 2. Of those that a mesh axis runs over, the one named last changes fastest.
Arguments:
- omega: float32 [3, 1024, 512, 128], P(None, 'gy', 'gz'), may hold values from -6 to 6
- velocity: float32 [3, 1024, 512, 128], P(None, 'gy', 'gz'), may hold values from -6 to 6
- point_owner: int32 [1152], replicated, may hold values from 2 to 477, as said below
- point_cells: int32 [3, 1152], replicated, may hold values from 1 to 125, as said below
- point_frac: float32 [3, 1152], replicated, may hold values from 0 to 1
- chord: float32 [1152], replicated, may hold values from 0.2 to 1
- twist: float32 [1152], replicated, may hold values from -0.3 to 0.3
- angle_step: int32 [1], replicated, may hold values from 0 to 719
Outputs:
- omega_out: float32 [3, 1024, 512, 128], P(None, 'gy', 'gz')
- blade_sources: float32 [3, 1152], replicated
Inputs may be any that keep to these rules, and one draw needn't show every extreme that they name: `point_owner`: turbine t's points lie in spanwise blocks t * 10 to (t + 1) * 10 - 1 and in the 4 vertical blocks from (4) // 2 on; no block holds more than 9 points, and in every turbine one block holds exactly 9. `point_cells`: streamwise cells lie in 1 to 125, spanwise in 1 to 13, vertical in 1 to 61; all points of a turbine share one streamwise cell.
All inputs are finite; a program needn't handle non-finite values.
Results may differ from a plain program's by a relative error of at most 0.0003.
Values sent between devices are 32-bit elements; how exact they have to be, the bound alone decides.
A program may use at most 128 MiB of HBM per device.

v0:
```python
import jax
import jax.numpy as jnp
from jax import lax
from jax.sharding import Mesh
from jax.sharding import PartitionSpec as P

TURBINES = 6
BLADES = 3
BP = 64
GY = ("gy_0", "gy_1", "gy_2")
GZ = ("gz_0", "gz_1")
GY_GZ = ("gy_0", "gy_1", "gy_2", "gz_0", "gz_1")
section_step = 0.4
viscosity = 0.05
tip_speed = 3.0
turn_step = 2.0 * 3.141592653589793 / 720.0


def by_axis(x, axes):
    for axis in axes:
        x = lax.psum(x, axis)
    return x


def with_halo(x, sides, width):
    edges = {}
    for axis, dim in sides:
        size, length = (lax.axis_size(axis), x.shape[dim])
        up = [(i, (i + 1) % size) for i in range(size - 1)]
        last = lax.slice_in_dim(x, length - width, length, axis=dim)
        initial = lax.slice_in_dim(x, 0, width, axis=dim)
        edges[dim] = (
            lax.ppermute(last, axis, up),
            lax.ppermute(initial, axis, [(b, a) for a, b in up]),
        )
    done = []
    for _, dim in sides:
        low, high = edges[dim]
        around = [(width, width) if d in done else (0, 0) for d in range(x.ndim)]
        x = jnp.concatenate([jnp.pad(low, around), x, jnp.pad(high, around)], axis=dim)
        done.append(dim)
    return x


def with_halo_2(x, sides, width):
    for axis, dim in sides:
        size, length = (lax.axis_size(axis), x.shape[dim])
        up = [(i, (i + 1) % size) for i in range(size - 1)]
        down = [(j, i) for i, j in up]
        last = lax.slice_in_dim(x, length - width, length, axis=dim)
        initial = lax.slice_in_dim(x, 0, width, axis=dim)
        before = lax.ppermute(last, axis, up)
        after = lax.ppermute(initial, axis, down)
        x = jnp.concatenate([before, x, after], axis=dim)
    return x


def remesh_kernel(shift):
    mag = jnp.abs(shift)
    inner = 1.0 - 2.5 * mag * mag + 1.5 * mag * mag * mag
    outer = 0.5 * (2.0 - mag) * (2.0 - mag) * (1.0 - mag)
    return jnp.where(mag < 1.0, inner, jnp.where(mag < 2.0, outer, 0.0))


def shifted(padded, axis, offset):
    index = []
    for dim in range(4):
        if dim == 0:
            index.append(slice(None))
        elif dim == axis:
            index.append(slice(offset, offset + padded.shape[dim] - 4))
        else:
            index.append(slice(2, padded.shape[dim] - 2))
    return padded[tuple(index)]


def centered_first(padded, axis):
    return (
        shifted(padded, axis, 0)
        - 8.0 * shifted(padded, axis, 1)
        + 8.0 * shifted(padded, axis, 3)
        - shifted(padded, axis, 4)
    ) / 12.0


def centered_second(padded, axis):
    return (
        -shifted(padded, axis, 0)
        + 16.0 * shifted(padded, axis, 1)
        - 30.0 * shifted(padded, axis, 2)
        + 16.0 * shifted(padded, axis, 3)
        - shifted(padded, axis, 4)
    ) / 12.0


def remesh_padded(field, displace, axis):
    length = field.shape[axis] - 4
    total = jnp.zeros(field.shape[:axis] + (length,) + field.shape[axis + 1 :], jnp.float32)
    for offset in range(-2, 3):
        start = 2 - offset
        part = lax.slice_in_dim(field, start, start + length, axis=axis)
        moved = lax.slice_in_dim(displace, start, start + length, axis=axis - 1)
        total = total + remesh_kernel(offset - moved)[None] * part
    return total


def blade_forces(point_velocity, chord, twist, angle_step):
    count = point_velocity.shape[1]
    points = jnp.arange(count, dtype=jnp.int32)
    station = points % BP
    blade = points // BP % BLADES
    theta = angle_step[0].astype(
        jnp.float32
    ) * turn_step + 2.0 * 3.141592653589793 / 3.0 * blade.astype(jnp.float32)
    radius = (station.astype(jnp.float32) + 0.5) / BP
    cos_t = jnp.cos(theta)
    sin_t = jnp.sin(theta)
    rel_x = point_velocity[0]
    rel_y = point_velocity[1] + tip_speed * radius * sin_t
    rel_z = point_velocity[2] - tip_speed * radius * cos_t
    rel_t = -sin_t * rel_y + cos_t * rel_z
    speed = jnp.sqrt(rel_x * rel_x + rel_t * rel_t + 1.0)
    gamma = 3.141592653589793 * chord * (rel_x * jnp.cos(twist) + rel_t * jnp.sin(twist))
    blades = gamma.reshape(-1, BP)
    before = jnp.concatenate([jnp.zeros((blades.shape[0], 1), jnp.float32), blades[:, :-1]], axis=1)
    shed = (blades - before).reshape(-1)
    return jnp.stack(
        [
            shed * rel_x / speed,
            gamma * cos_t + shed * rel_y / speed,
            gamma * sin_t + shed * rel_z / speed,
        ]
    )


def point_tables(
    cells,
    fracs,
    owner_span,
    owner_vert,
    span_index,
    vert_index,
    span_cells,
    vert_cells,
    axial_cells,
):
    rows_x = jnp.arange(axial_cells, dtype=jnp.int32)
    rows_y = jnp.arange(span_cells, dtype=jnp.int32)
    rows_z = jnp.arange(vert_cells, dtype=jnp.int32)
    gap_x = rows_x[:, None] - cells[0][None, :]
    gap_y = (
        span_index * span_cells
        + rows_y[:, None]
        - owner_span[None, :] * span_cells
        - cells[1][None, :]
    )
    gap_z = (
        vert_index * vert_cells
        + rows_z[:, None]
        - owner_vert[None, :] * vert_cells
        - cells[2][None, :]
    )
    table_x = remesh_kernel(gap_x.astype(jnp.float32) - fracs[0][None, :])
    table_y = remesh_kernel(gap_y.astype(jnp.float32) - fracs[1][None, :])
    table_z = remesh_kernel(gap_z.astype(jnp.float32) - fracs[2][None, :])
    return (table_x, table_y, table_z)


def on_device(omega, velocity, point_owner, point_cells, point_frac, chord, twist, angle_step):
    span_cells, vert_cells, axial_cells = (omega.shape[1], omega.shape[2], omega.shape[3])
    span_count = lax.axis_size(GY)
    vert_count = lax.axis_size(GZ)
    span_index = lax.axis_index(GY)
    vert_index = lax.axis_index(GZ)
    owner_span = point_owner // vert_count
    owner_vert = point_owner % vert_count
    highest = lax.Precision.HIGHEST
    busiest = 2 * (BLADES * BP) // (span_count // TURBINES * max(vert_count // 2, 1))
    my_block = span_index * vert_count + vert_index
    points = jnp.arange(point_owner.shape[0], dtype=jnp.int32)
    ranking = jnp.where(point_owner == my_block, points, points + point_owner.shape[0])
    picked = jnp.argsort(ranking, stable=True)[:busiest]
    selector = (picked[:, None] == points[None, :]).astype(jnp.float32)
    table_x, table_y, table_z = point_tables(
        point_cells[:, picked],
        point_frac[:, picked],
        owner_span[picked],
        owner_vert[picked],
        span_index,
        vert_index,
        span_cells,
        vert_cells,
        axial_cells,
    )
    columns = jnp.dot(
        velocity.reshape(-1, axial_cells),
        table_x,
        precision=highest,
        preferred_element_type=jnp.float32,
    )
    columns = columns.reshape(3, span_cells, vert_cells, -1)
    compact = jnp.einsum("cyzq,yq,zq->cq", columns, table_y, table_z, precision=highest)
    partial_velocity = jnp.dot(
        compact, selector, precision=highest, preferred_element_type=jnp.float32
    )
    point_velocity = by_axis(partial_velocity, GY_GZ)
    sources = blade_forces(point_velocity, chord, twist, angle_step)
    local_sources = sources[:, picked]
    spread = jnp.einsum("cq,yq,zq->cyzq", local_sources, table_y, table_z, precision=highest)
    smear = jnp.dot(
        spread.reshape(-1, spread.shape[3]),
        table_x.T,
        precision=highest,
        preferred_element_type=jnp.float32,
    )
    smear = smear.reshape(3, span_cells, vert_cells, axial_cells)
    omega_rim, velocity_rim = (
        with_halo(omega, ((GY, 1), (GZ, 2)), 2),
        with_halo(velocity, ((GY, 1), (GZ, 2)), 2),
    )
    axial_pads = ((0, 0), (0, 0), (0, 0), (2, 2))
    omega_pad = jnp.pad(omega_rim, axial_pads)
    velocity_pad = jnp.pad(velocity_rim, axial_pads)
    stretch = jnp.zeros_like(omega)
    laplace = jnp.zeros_like(omega)
    for axis in range(3):
        stretch = stretch + omega[2 - axis][None] * centered_first(velocity_pad, 3 - axis)
        laplace = laplace + centered_second(omega_pad, axis + 1)
    section = omega + section_step * (stretch + viscosity * laplace + smear)
    shift_x = jnp.clip(section_step * velocity[0], -1.0, 1.0)
    moved_x = remesh_padded(
        jnp.pad(section, axial_pads), jnp.pad(shift_x, ((0, 0), (0, 0), (2, 2))), 3
    )
    shift_z = jnp.clip(section_step * velocity_rim[2][2 : span_cells + 2, :, :], -1.0, 1.0)
    span_rim = with_halo_2(moved_x, ((GY, 1),), 2)
    shift_y = jnp.clip(section_step * velocity_rim[1][:, 2 : vert_cells + 2, :], -1.0, 1.0)
    moved_mid = remesh_padded(span_rim, shift_y, 1)
    moved_y = with_halo_2(moved_mid, ((GZ, 2),), 2)
    omega_out = remesh_padded(moved_y, shift_z, 2)
    return (omega_out, sources)


def solution(mesh):
    split = Mesh(mesh.devices.reshape(8, 4, 2, 2, 4), ("gy_0", "gy_1", "gy_2", "gz_0", "gz_1"))
    placed = (P(None, GY, GZ, None), P(None, GY, GZ, None), P(), P(), P(), P(), P(), P())
    return jax.shard_map(
        on_device,
        mesh=split,
        in_specs=placed,
        out_specs=(P(None, GY, GZ, None), P()),
        check_vma=False,
    )
```

profile of v0, /device:TPU:96, one launch (start us, length us, event | category | flops | bytes accessed | tf_op | source)
XLA Modules:
  0.0 213.7 jit_solution(1090650749825777599)
XLA Ops:
  0.7 1.9 fusion.256
  2.6 1.9 collective-permute-start.1
  4.5 1.8 fusion.258
  6.3 2.7 %collective-permute-start.4 = (f32[3,2,64,128]{3,2,1,0:T(8,128)}, f32[3,2,64,128]{3,2,1,0:T(8,128)}, u32[]{:S(2)}, u32[]{:S(2)}) collective-permute-start(f32[3,2,64,128]{3,2,1,0:T(8,128)} %get-tuple-element.35), channel_id=1, source_target_pairs={{0,8},{8,16},{16,24},{24,32},{32,40},{40,48},{48,56},{56,64},{64,7... | collective-permute-start | bytes 589832 | tf_op jit(solution)/shard_map/ppermute | solution.py:33
  9.0 0.7 fusion.255
  9.7 3.4 %collective-permute-start = (f32[3,16,2,128]{3,2,1,0:T(2,128)}, f32[3,16,2,128]{3,2,1,0:T(2,128)}, u32[]{:S(2)}, u32[]{:S(2)}) collective-permute-start(f32[3,16,2,128]{3,2,1,0:T(2,128)} %get-tuple-element.28), channel_id=1, source_target_pairs={{0,1},{1,2},{2,3},{3,4},{4,5},{5,6},{6,7},{8,9},{9,10},{10,11},{11... | collective-permute-start | bytes 147464 | tf_op jit(solution)/shard_map/ppermute | solution.py:33
  13.1 8.5 %collective-permute-start.3 = (f32[3,16,2,128]{3,2,1,0:T(2,128)}, f32[3,16,2,128]{3,2,1,0:T(2,128)S(1)}, u32[]{:S(2)}, u32[]{:S(2)}) collective-permute-start(f32[3,16,2,128]{3,2,1,0:T(2,128)} %get-tuple-element.29), channel_id=1, source_target_pairs={{1,0},{2,1},{3,2},{4,3},{5,4},{6,5},{7,6},{9,8},{10,9},{11,10},{12... | collective-permute-start | bytes 147464 | tf_op jit(solution)/shard_map/ppermute | solution.py:34
  21.6 1.7 fusion.257
  23.3 1.9 collective-permute-start.6
  25.3 5.0 %sort.17 = (s32[1152]{0:T(1024)}, s32[1152]{0:T(1024)S(1)}) sort(s32[1152]{0:T(1024)S(1)} %get-tuple-element.61, s32[1152]{0:T(1024)S(1)} %iota.43), dimensions={0}, to_apply=%region_0.1 | sort | flops 12672 | bytes 18432 | tf_op jit(solution)/shard_map/jit(argsort)/sort | solution.py:182
  30.3 0.5 fusion.259
  30.8 0.7 gather_fusion.3
  31.5 0.2 copy.15
  31.7 0.6 gather_fusion.2
  32.3 0.2 slice_reduce_fusion.2
  32.5 0.2 copy.14
  32.8 0.6 gather_fusion.1
  33.3 0.2 slice_reduce_fusion.3
  33.6 2.1 convolution_bitcast_fusion
  35.7 1.0 reshape.177
  36.7 0.7 gather_fusion
  37.4 0.1 fusion.240
  37.5 0.1 copy.20
  37.5 0.7 fusion.234
  38.2 1.2 fusion.231
  39.5 0.2 fusion.174
  39.7 0.9 fusion.172
  40.6 32.1 %psum.35 = f32[3,1152]{1,0:T(4,128)S(1)} all-reduce(f32[3,1152]{1,0:T(4,128)S(1)} %fusion.172), channel_id=1, replica_groups=mesh['gy_0'=8,'gy_1'=4,'gy_2'=2,'gz_0'=2,'gz_1'=4] {'gy_0'}, use_global_device_ids=true, to_apply=%region_1.2 | all-reduce | flops 3456 | bytes 27648 | tf_op jit(solution)/shard_map/psum | solution.py:21
  72.7 19.3 %psum.36 = f32[3,1152]{1,0:T(4,128)S(1)} all-reduce(f32[3,1152]{1,0:T(4,128)S(1)} %psum.35), channel_id=1, replica_groups=mesh['gy_0'=8,'gy_1'=4,'gy_2'=2,'gz_0'=2,'gz_1'=4] {'gy_1'}, use_global_device_ids=true, to_apply=%region_2.3 | all-reduce | flops 3456 | bytes 27648 | tf_op jit(solution)/shard_map/psum | solution.py:21
  91.9 3.4 %psum.37 = f32[3,1152]{1,0:T(4,128)S(1)} all-reduce(f32[3,1152]{1,0:T(4,128)S(1)} %psum.36), channel_id=1, replica_groups=mesh['gy_0'=8,'gy_1'=4,'gy_2'=2,'gz_0'=2,'gz_1'=4] {'gy_2'}, use_global_device_ids=true, to_apply=%region_3.4 | all-reduce | flops 3456 | bytes 27648 | tf_op jit(solution)/shard_map/psum | solution.py:21
  95.3 10.7 %psum.38 = f32[3,1152]{1,0:T(4,128)S(1)} all-reduce(f32[3,1152]{1,0:T(4,128)S(1)} %psum.37), channel_id=1, replica_groups=mesh['gy_0'=8,'gy_1'=4,'gy_2'=2,'gz_0'=2,'gz_1'=4] {'gz_0'}, use_global_device_ids=true, to_apply=%region_4.5 | all-reduce | flops 3456 | bytes 27648 | tf_op jit(solution)/shard_map/psum | solution.py:21
  106.1 22.9 %psum.39 = f32[3,1152]{1,0:T(4,128)S(1)} all-reduce(f32[3,1152]{1,0:T(4,128)S(1)} %psum.38), channel_id=1, replica_groups=mesh['gy_0'=8,'gy_1'=4,'gy_2'=2,'gz_0'=2,'gz_1'=4] {'gz_1'}, use_global_device_ids=true, to_apply=%region_5.6 | all-reduce | flops 3456 | bytes 27648 | tf_op jit(solution)/shard_map/psum | solution.py:21
  129.6 0.1 add_multiply_fusion
  130.0 1.2 multiply_bitcast_fusion.2
  131.3 1.2 fusion.96
  132.5 0.2 rsqrt_multiply_fusion
  132.8 2.6 %fusion.85 = (f32[16,64,128]{2,1,0:T(8,128)}, f32[16,64,128]{2,1,0:T(8,128)}, f32[16,64,128]{2,1,0:T(8,128)}, f32[16,64,128]{2,1,0:T(8,128)}) fusion(f32[16,64,128]{2,1,0:T(8,128)S(1)} %get-tuple-element.18), kind=kLoop, calls=%fused_computation.191 | loop fusion | flops 9437184 | bytes 2621440 | tf_op jit(solution)/shard_map/jit(_where)/select_n | solution.py:62
  135.4 1.1 copy.16
  136.4 1.6 gather_fusion.4
  138.1 0.1 copy.17
  138.2 1.9 collective-permute-start.7
  140.1 0.8 pad.29
  140.9 1.9 collective-permute-start.2
  142.9 3.3 %collective-permute-start.5 = (f32[3,2,64,128]{3,2,1,0:T(8,128)}, f32[3,2,64,128]{3,2,1,0:T(8,128)S(1)}, u32[]{:S(2)}, u32[]{:S(2)}) collective-permute-start(f32[3,2,64,128]{3,2,1,0:T(8,128)} %get-tuple-element.34), channel_id=1, source_target_pairs={{8,0},{16,8},{24,16},{32,24},{40,32},{48,40},{56,48},{64,56},{72,6... | collective-permute-start | bytes 589832 | tf_op jit(solution)/shard_map/ppermute | solution.py:34
  146.3 1.0 constant_dynamic-update-slice_fusion.4
  147.3 1.0 constant_dynamic-update-slice_fusion.8
  148.2 1.2 constant_dynamic-update-slice_fusion.3
  149.5 0.3 pad_maximum_fusion
  149.9 1.0 copy-done.5
  151.0 3.7 %select_maximum_fusion = f32[3,20,68,132]{3,2,1,0:T(8,128)} fusion(f32[3,20,2,128]{3,2,1,0:T(2,128)S(1)} %pad.34, f32[3,20,64,128]{3,2,1,0:T(8,128)S(1)} %get-tuple-element.57, f32[3,20,2,128]{3,2,1,0:T(2,128)S(1)} %pad.33), kind=kLoop, calls=%fused_computation.15 | loop fusion | flops 4308480 | bytes 4243200 | tf_op jit(solution)/shard_map/concatenate | solution.py:40
  154.8 19.1 %fusion.27 = f32[3,16,64,128]{3,2,1,0:T(8,128)} fusion(f32[3,16,64,128]{3,2,1,0:T(8,128)S(1)} %copy-done.1, f32[3,20,64,128]{3,2,1,0:T(8,128)} %copy-done.3, f32[3,20,2,128]{3,2,1,0:T(2,128)S(1)} %pad.34, f32[3,20,2,128]{3,2,1,0:T(2,128)S(1)} %pad.33, f32[3,20,64,128]{3,2,1,0:T(8,128)} %copy-done.2, f32[3,20,2,128]{3,2,1,0:T(2,128)S(1)} %pad.30, ...), kind=kOutput, calls=%fused_computation.66 | convolution fusion | flops 64931328 | bytes 29863944 | tf_op jit(solution)/shard_map/dot_general | solution.py:210
  173.9 6.4 %fusion.45 = f32[3,16,64,128]{3,2,1,0:T(8,128)S(1)} fusion(f32[3,16,64,128]{3,2,1,0:T(8,128)} %fusion.27, f32[16,64,128]{2,1,0:T(8,128)} %get-tuple-element.49, f32[16,64,128]{2,1,0:T(8,128)} %get-tuple-element.48, f32[16,64,128]{2,1,0:T(8,128)} %get-tuple-element.17, f32[16,64,128]{2,1,0:T(8,128)} %get-tuple-element.47, f32[16,64,128]{2,1,0:T(8,128)} %get-tuple-element.46), kind=kLoop, calls=%fused_computation.84 | loop fusion | flops 3538944 | bytes 5767168 | tf_op jit(solution)/shard_map/add | solution.py:103
  180.3 4.8 %collective-permute-start.8 = (f32[3,2,64,128]{3,2,1,0:T(8,128)S(1)}, f32[3,2,64,128]{3,2,1,0:T(8,128)S(1)}, u32[]{:S(2)}, u32[]{:S(2)}) collective-permute-start(f32[3,2,64,128]{3,2,1,0:T(8,128)S(1)} %get-tuple-element.15), channel_id=1, source_target_pairs={{8,0},{16,8},{24,16},{32,24},{40,32},{48,40},{56,48},{64,56},{72,6... | collective-permute-start | bytes 589832 | tf_op jit(solution)/shard_map/ppermute | solution.py:53
  185.1 1.9 collective-permute-start.9
  187.0 0.1 fusion.70
  187.1 1.5 fusion.80
  188.8 1.2 collective-permute-done.8
  189.9 4.9 %collective-permute-done.9 = f32[3,2,64,128]{3,2,1,0:T(8,128)S(1)} collective-permute-done((f32[3,2,64,128]{3,2,1,0:T(8,128)S(1)}, f32[3,2,64,128]{3,2,1,0:T(8,128)S(1)}, u32[]{:S(2)}, u32[]{:S(2)}) %collective-permute-start.9) | collective-permute-done | bytes 196640 | tf_op jit(solution)/shard_map/ppermute | solution.py:52
  194.8 1.3 fusion.12
  196.2 3.4 %collective-permute-start.10 = (f32[3,16,2,128]{3,2,1,0:T(2,128)S(1)}, f32[3,16,2,128]{3,2,1,0:T(2,128)S(1)}, u32[]{:S(2)}, u32[]{:S(2)}) collective-permute-start(f32[3,16,2,128]{3,2,1,0:T(2,128)S(1)} %get-tuple-element.13), channel_id=1, source_target_pairs={{1,0},{2,1},{3,2},{4,3},{5,4},{6,5},{7,6},{9,8},{10,9},{11,10},{12... | collective-permute-start | bytes 147464 | tf_op jit(solution)/shard_map/ppermute | solution.py:53
  199.6 2.4 %collective-permute-start.11 = (f32[3,16,2,128]{3,2,1,0:T(2,128)S(1)}, f32[3,16,2,128]{3,2,1,0:T(2,128)S(1)}, u32[]{:S(2)}, u32[]{:S(2)}) collective-permute-start(f32[3,16,2,128]{3,2,1,0:T(2,128)S(1)} %get-tuple-element.14), channel_id=1, source_target_pairs={{0,1},{1,2},{2,3},{3,4},{4,5},{5,6},{6,7},{8,9},{9,10},{10,11},{11... | collective-permute-start | bytes 147464 | tf_op jit(solution)/shard_map/ppermute | solution.py:52
  202.0 1.7 fusion.75
  203.7 7.9 %collective-permute-done.11 = f32[3,16,2,128]{3,2,1,0:T(2,128)S(1)} collective-permute-done((f32[3,16,2,128]{3,2,1,0:T(2,128)S(1)}, f32[3,16,2,128]{3,2,1,0:T(2,128)S(1)}, u32[]{:S(2)}, u32[]{:S(2)}) %collective-permute-start.11) | collective-permute-done | bytes 49184 | tf_op jit(solution)/shard_map/ppermute | solution.py:52
  211.6 2.1 fusion.4
  (70 shorter events, 0.9 us)
Async XLA Ops:
  0.6 8.4 %copy-start = (f32[3,16,64,128]{3,2,1,0:T(8,128)S(1)}, f32[3,16,64,128]{3,2,1,0:T(8,128)}, u32[]{:S(2)}) copy-start(f32[3,16,64,128]{3,2,1,0:T(8,128)} %param.9) | copy-start | bytes 4718596
  0.6 24.6 %copy-start.15 = (s32[1152]{0:T(1024)S(1)}, s32[1152]{0:T(1024)}, u32[]{:S(2)}) copy-start(s32[1152]{0:T(1024)} %param.10) | copy-start | bytes 13828
  0.7 30.8 %copy-start.10 = (f32[3,1152]{1,0:T(4,128)S(1)}, f32[3,1152]{1,0:T(4,128)}, u32[]{:S(2)}) copy-start(f32[3,1152]{1,0:T(4,128)} %param.12) | copy-start | bytes 41476
  0.7 31.8 %copy-start.11 = (s32[3,1152]{1,0:T(4,128)S(1)}, s32[3,1152]{1,0:T(4,128)}, u32[]{:S(2)}) copy-start(s32[3,1152]{1,0:T(4,128)} %param.11) | copy-start | bytes 41476
  2.6 143.7 %collective-permute-start.1 = (f32[3,2,64,128]{3,2,1,0:T(8,128)}, f32[3,2,64,128]{3,2,1,0:T(8,128)}, u32[]{:S(2)}, u32[]{:S(2)}) collective-permute-start(f32[3,2,64,128]{3,2,1,0:T(8,128)} %get-tuple-element.31), channel_id=1, source_target_pairs={{0,8},{8,16},{16,24},{24,32},{32,40},{40,48},{48,56},{56,64},{64,7... | collective-permute-start | bytes 589832 | tf_op jit(solution)/shard_map/ppermute | solution.py:33
  6.3 140.9 %collective-permute-start.4 = (f32[3,2,64,128]{3,2,1,0:T(8,128)}, f32[3,2,64,128]{3,2,1,0:T(8,128)}, u32[]{:S(2)}, u32[]{:S(2)}) collective-permute-start(f32[3,2,64,128]{3,2,1,0:T(8,128)} %get-tuple-element.35), channel_id=1, source_target_pairs={{0,8},{8,16},{16,24},{24,32},{32,40},{40,48},{48,56},{56,64},{64,7... | collective-permute-start | bytes 589832 | tf_op jit(solution)/shard_map/ppermute | solution.py:33
  9.7 128.4 %collective-permute-start = (f32[3,16,2,128]{3,2,1,0:T(2,128)}, f32[3,16,2,128]{3,2,1,0:T(2,128)}, u32[]{:S(2)}, u32[]{:S(2)}) collective-permute-start(f32[3,16,2,128]{3,2,1,0:T(2,128)} %get-tuple-element.28), channel_id=1, source_target_pairs={{0,1},{1,2},{2,3},{3,4},{4,5},{5,6},{6,7},{8,9},{9,10},{10,11},{11... | collective-permute-start | bytes 147464 | tf_op jit(solution)/shard_map/ppermute | solution.py:33
  13.1 127.8 %collective-permute-start.3 = (f32[3,16,2,128]{3,2,1,0:T(2,128)}, f32[3,16,2,128]{3,2,1,0:T(2,128)S(1)}, u32[]{:S(2)}, u32[]{:S(2)}) collective-permute-start(f32[3,16,2,128]{3,2,1,0:T(2,128)} %get-tuple-element.29), channel_id=1, source_target_pairs={{1,0},{2,1},{3,2},{4,3},{5,4},{6,5},{7,6},{9,8},{10,9},{11,10},{12... | collective-permute-start | bytes 147464 | tf_op jit(solution)/shard_map/ppermute | solution.py:34
  23.3 119.6 %collective-permute-start.6 = (f32[3,16,2,128]{3,2,1,0:T(2,128)}, f32[3,16,2,128]{3,2,1,0:T(2,128)S(1)}, u32[]{:S(2)}, u32[]{:S(2)}) collective-permute-start(f32[3,16,2,128]{3,2,1,0:T(2,128)} %get-tuple-element.32), channel_id=1, source_target_pairs={{0,1},{1,2},{2,3},{3,4},{4,5},{5,6},{6,7},{8,9},{9,10},{10,11},{11... | collective-permute-start | bytes 147464 | tf_op jit(solution)/shard_map/ppermute | solution.py:33
  33.5 39.2 %copy-start.16 = (s32[9]{0:T(128)}, s32[9]{0:T(128)S(1)}, u32[]{:S(2)}) copy-start(s32[9]{0:T(128)S(1)} %get-tuple-element.7) | copy-start | bytes 112
  33.5 96.1 %copy-start.12 = (f32[1152]{0:T(1024)S(1)}, f32[1152]{0:T(1024)}, u32[]{:S(2)}) copy-start(f32[1152]{0:T(1024)} %param.14) | copy-start | bytes 13828
  33.5 96.1 %copy-start.13 = (f32[1152]{0:T(1024)S(1)}, f32[1152]{0:T(1024)}, u32[]{:S(2)}) copy-start(f32[1152]{0:T(1024)} %param.13) | copy-start | bytes 13828
  33.6 96.5 %copy-start.1 = (f32[3,16,64,128]{3,2,1,0:T(8,128)S(1)}, f32[3,16,64,128]{3,2,1,0:T(8,128)}, u32[]{:S(2)}) copy-start(f32[3,16,64,128]{3,2,1,0:T(8,128)} %param.8) | copy-start | bytes 4718596
  132.7 5.4 %copy-start.7 = (f32[3,16,2,128]{3,2,1,0:T(2,128)S(1)}, f32[3,16,2,128]{3,2,1,0:T(2,128)}, u32[]{:S(2)}) copy-start(f32[3,16,2,128]{3,2,1,0:T(2,128)} %get-tuple-element.33) | copy-start | bytes 147460
  135.4 14.1 %copy-start.6 = (f32[3,1152]{1,0:T(4,128)}, f32[3,1152]{1,0:T(4,128)S(1)}, u32[]{:S(2)}) copy-start(f32[3,1152]{1,0:T(4,128)S(1)} %pad_maximum_fusion.9) | copy-start | bytes 41476
  138.2 8.1 %collective-permute-start.7 = (f32[3,16,2,128]{3,2,1,0:T(2,128)S(1)}, f32[3,16,2,128]{3,2,1,0:T(2,128)S(1)}, u32[]{:S(2)}, u32[]{:S(2)}) collective-permute-start(f32[3,16,2,128]{3,2,1,0:T(2,128)S(1)} %copy-done.7), channel_id=1, source_target_pairs={{1,0},{2,1},{3,2},{4,3},{5,4},{6,5},{7,6},{9,8},{10,9},{11,10},{12... | collective-permute-start | bytes 147464 | tf_op jit(solution)/shard_map/ppermute | solution.py:34
  140.9 8.5 %collective-permute-start.2 = (f32[3,2,64,128]{3,2,1,0:T(8,128)}, f32[3,2,64,128]{3,2,1,0:T(8,128)S(1)}, u32[]{:S(2)}, u32[]{:S(2)}) collective-permute-start(f32[3,2,64,128]{3,2,1,0:T(8,128)} %get-tuple-element.30), channel_id=1, source_target_pairs={{8,0},{16,8},{24,16},{32,24},{40,32},{48,40},{56,48},{64,56},{72,6... | collective-permute-start | bytes 589832 | tf_op jit(solution)/shard_map/ppermute | solution.py:34
  142.9 8.0 %collective-permute-start.5 = (f32[3,2,64,128]{3,2,1,0:T(8,128)}, f32[3,2,64,128]{3,2,1,0:T(8,128)S(1)}, u32[]{:S(2)}, u32[]{:S(2)}) collective-permute-start(f32[3,2,64,128]{3,2,1,0:T(8,128)} %get-tuple-element.34), channel_id=1, source_target_pairs={{8,0},{16,8},{24,16},{32,24},{40,32},{48,40},{56,48},{64,56},{72,6... | collective-permute-start | bytes 589832 | tf_op jit(solution)/shard_map/ppermute | solution.py:34
  149.4 5.3 %copy-start.8 = (f32[3,18,64,128]{3,2,1,0:T(8,128)}, f32[3,18,64,128]{3,2,1,0:T(8,128)S(1)}, u32[]{:S(2)}) copy-start(f32[3,18,64,128]{3,2,1,0:T(8,128)S(1)} %get-tuple-element.22) | copy-start | bytes 5308420
  149.5 5.3 %copy-start.9 = (f32[3,18,64,128]{3,2,1,0:T(8,128)}, f32[3,18,64,128]{3,2,1,0:T(8,128)S(1)}, u32[]{:S(2)}) copy-start(f32[3,18,64,128]{3,2,1,0:T(8,128)S(1)} %get-tuple-element.71) | copy-start | bytes 5308420
  149.5 1.4 copy-start.5
  149.5 5.2 %copy-start.2 = (f32[3,20,64,128]{3,2,1,0:T(8,128)}, f32[3,20,64,128]{3,2,1,0:T(8,128)S(1)}, u32[]{:S(2)}) copy-start(f32[3,20,64,128]{3,2,1,0:T(8,128)S(1)} %get-tuple-element.53) | copy-start | bytes 5898244
  151.0 3.8 %copy-start.4 = (f32[3,18,64,128]{3,2,1,0:T(8,128)}, f32[3,18,64,128]{3,2,1,0:T(8,128)S(1)}, u32[]{:S(2)}) copy-start(f32[3,18,64,128]{3,2,1,0:T(8,128)S(1)} %get-tuple-element.56) | copy-start | bytes 5308420
  151.0 3.8 %copy-start.3 = (f32[3,20,64,128]{3,2,1,0:T(8,128)}, f32[3,20,64,128]{3,2,1,0:T(8,128)S(1)}, u32[]{:S(2)}) copy-start(f32[3,20,64,128]{3,2,1,0:T(8,128)S(1)} %get-tuple-element.57) | copy-start | bytes 5898244
  151.0 3.8 %copy-start.14 = (f32[9,64]{1,0:T(8,128)S(1)}, f32[9,64]{1,0:T(8,128)}, u32[]{:S(2)}) copy-start(f32[9,64]{1,0:T(8,128)} %get-tuple-element.68) | copy-start | bytes 6916
  151.0 3.8 %copy-start.17 = (s32[9]{0:T(128)S(1)}, s32[9]{0:T(128)}, u32[]{:S(2)}) copy-start(s32[9]{0:T(128)} %copy-done.16) | copy-start | bytes 112
  180.3 9.6 %collective-permute-start.8 = (f32[3,2,64,128]{3,2,1,0:T(8,128)S(1)}, f32[3,2,64,128]{3,2,1,0:T(8,128)S(1)}, u32[]{:S(2)}, u32[]{:S(2)}) collective-permute-start(f32[3,2,64,128]{3,2,1,0:T(8,128)S(1)} %get-tuple-element.15), channel_id=1, source_target_pairs={{8,0},{16,8},{24,16},{32,24},{40,32},{48,40},{56,48},{64,56},{72,6... | collective-permute-start | bytes 589832 | tf_op jit(solution)/shard_map/ppermute | solution.py:53
  185.1 9.7 %collective-permute-start.9 = (f32[3,2,64,128]{3,2,1,0:T(8,128)S(1)}, f32[3,2,64,128]{3,2,1,0:T(8,128)S(1)}, u32[]{:S(2)}, u32[]{:S(2)}) collective-permute-start(f32[3,2,64,128]{3,2,1,0:T(8,128)S(1)} %get-tuple-element.16), channel_id=1, source_target_pairs={{0,8},{8,16},{16,24},{24,32},{32,40},{40,48},{48,56},{56,64},{64,7... | collective-permute-start | bytes 589832 | tf_op jit(solution)/shard_map/ppermute | solution.py:52
  196.2 7.5 %collective-permute-start.10 = (f32[3,16,2,128]{3,2,1,0:T(2,128)S(1)}, f32[3,16,2,128]{3,2,1,0:T(2,128)S(1)}, u32[]{:S(2)}, u32[]{:S(2)}) collective-permute-start(f32[3,16,2,128]{3,2,1,0:T(2,128)S(1)} %get-tuple-element.13), channel_id=1, source_target_pairs={{1,0},{2,1},{3,2},{4,3},{5,4},{6,5},{7,6},{9,8},{10,9},{11,10},{12... | collective-permute-start | bytes 147464 | tf_op jit(solution)/shard_map/ppermute | solution.py:53
  199.6 12.0 %collective-permute-start.11 = (f32[3,16,2,128]{3,2,1,0:T(2,128)S(1)}, f32[3,16,2,128]{3,2,1,0:T(2,128)S(1)}, u32[]{:S(2)}, u32[]{:S(2)}) collective-permute-start(f32[3,16,2,128]{3,2,1,0:T(2,128)S(1)} %get-tuple-element.14), channel_id=1, source_target_pairs={{0,1},{1,2},{2,3},{3,4},{4,5},{5,6},{6,7},{8,9},{9,10},{10,11},{11... | collective-permute-start | bytes 147464 | tf_op jit(solution)/shard_map/ppermute | solution.py:52
where the time goes:
time: 214 us
  blocking collectives  88.4 us (41%)
  starting transfers between devices  38 us (18%)
  other arithmetic  29.1 us (14%)
  matrix products  23.5 us (11%)
  local copies, waits for them, and re-layouts  18.8 us (9%)
  waiting for transfers between devices  13.9 us (6%)
    psum x5, blocking collectives, by_axis(): x = lax.psum(x, axis)  88.4 us
    dot_general x1, matrix products, on_device(): jnp.dot(spread.reshape(-1, spread.shape[3]), table_x.T, precision=highest...  19.1 us
    ppermute x4, starting transfers between devices, with_halo(): lax.ppermute(initial, axis, [(b, a) for a, b in up])  15.6 us
    ppermute x2, waiting for transfers between devices, with_halo_2(): before = lax.ppermute(last, axis, up)  12.7 us
    ppermute x4, starting transfers between devices, with_halo(): lax.ppermute(last, axis, up)  9.88 us
    add x3, other arithmetic, remesh_padded(): total = total + remesh_kernel(offset - moved)[None] * part  9.84 us
    ppermute x2, starting transfers between devices, with_halo_2(): after = lax.ppermute(initial, axis, down)  8.16 us
    select_n x5, other arithmetic, remesh_kernel(): return jnp.where(mag < 1.0, inner, jnp.where(mag < 2.0, outer, 0.0))  6.53 us
  transfers between devices with their start and end apart: 12, of which 3 were waited for; matrix products, arithmetic and copies ran while one was open for 17% of the time, Pallas kernels for 0%

commit v1 on v0

--- a/solution.py
+++ b/solution.py
@@ -18,7 +18,7 @@
 
 def by_axis(x, axes):
     for axis in axes:
-        x = lax.psum(x, axis)
+        x = jnp.sum(lax.all_gather(x, axis), axis=0)
     return x
 
 

time: 214 us -> 201 us (0.939)
  blocking collectives: 88.4 us -> 65.3 us
  starting transfers between devices: 38 us -> 49 us
    psum x5 -> x0, blocking collectives: 88.4 us -> none  [by_axis(): x = lax.psum(x, axis)]
    all_gather x0 -> x5, blocking collectives: none -> 65.3 us  [by_axis(): x = jnp.sum(lax.all_gather(x, axis), axis=0)]
    ppermute x4, starting transfers between devices: 15.6 us -> 26.6 us  [with_halo(): lax.ppermute(initial, axis, [(b, a) for a, b in up])]
  transfers between devices with their start and end apart: 12 -> 12, of which waited for: 3 -> 3; matrix products, arithmetic and copies ran while one was open for 17% -> 18% of each run, Pallas kernels for 0% -> 0%
where the time goes in v1:
time: 201 us; the launch traced here: 200 us
  blocking collectives  65.3 us (32%)
  starting transfers between devices  49 us (24%)
  other arithmetic  29.2 us (15%)
  matrix products  23.5 us (12%)
  local copies, waits for them, and re-layouts  19 us (9%)
  waiting for transfers between devices  12.5 us (6%)
    all_gather x5, blocking collectives, by_axis(): x = jnp.sum(lax.all_gather(x, axis), axis=0)  65.3 us
    ppermute x4, starting transfers between devices, with_halo(): lax.ppermute(initial, axis, [(b, a) for a, b in up])  26.6 us
    dot_general x1, matrix products, on_device(): jnp.dot(spread.reshape(-1, spread.shape[3]), table_x.T, precision=highest...  19.1 us
    ppermute x2, waiting for transfers between devices, with_halo_2(): before = lax.ppermute(last, axis, up)  12 us
    ppermute x4, starting transfers between devices, with_halo(): lax.ppermute(last, axis, up)  9.88 us
    add x3, other arithmetic, remesh_padded(): total = total + remesh_kernel(offset - moved)[None] * part  9.84 us
    ppermute x2, starting transfers between devices, with_halo_2(): after = lax.ppermute(initial, axis, down)  6.69 us
    select_n x5, other arithmetic, remesh_kernel(): return jnp.where(mag < 1.0, inner, jnp.where(mag < 2.0, outer, 0.0))  6.52 us
  transfers between devices with their start and end apart: 12, of which 3 were waited for; matrix products, arithmetic and copies ran while one was open for 18% of the time, Pallas kernels for 0%

profile of v1, /device:TPU:96, one launch (start us, length us, event | category | flops | bytes accessed | tf_op | source)
XLA Modules:
  0.0 200.3 jit_solution(15446815508385143966)
XLA Ops:
  0.7 1.9 fusion.255
  2.6 1.9 collective-permute-start.1
  4.5 1.8 fusion.257
  6.3 2.7 %collective-permute-start.4 = (f32[3,2,64,128]{3,2,1,0:T(8,128)}, f32[3,2,64,128]{3,2,1,0:T(8,128)}, u32[]{:S(2)}, u32[]{:S(2)}) collective-permute-start(f32[3,2,64,128]{3,2,1,0:T(8,128)} %get-tuple-element.39), channel_id=1, source_target_pairs={{0,8},{8,16},{16,24},{24,32},{32,40},{40,48},{48,56},{56,64},{64,7... | collective-permute-start | bytes 589832 | tf_op jit(solution)/shard_map/ppermute | solution.py:33
  9.0 0.7 fusion.254
  9.7 3.4 %collective-permute-start = (f32[3,16,2,128]{3,2,1,0:T(2,128)}, f32[3,16,2,128]{3,2,1,0:T(2,128)}, u32[]{:S(2)}, u32[]{:S(2)}) collective-permute-start(f32[3,16,2,128]{3,2,1,0:T(2,128)} %get-tuple-element.32), channel_id=1, source_target_pairs={{0,1},{1,2},{2,3},{3,4},{4,5},{5,6},{6,7},{8,9},{9,10},{10,11},{11... | collective-permute-start | bytes 147464 | tf_op jit(solution)/shard_map/ppermute | solution.py:33
  13.1 8.5 %collective-permute-start.3 = (f32[3,16,2,128]{3,2,1,0:T(2,128)}, f32[3,16,2,128]{3,2,1,0:T(2,128)S(1)}, u32[]{:S(2)}, u32[]{:S(2)}) collective-permute-start(f32[3,16,2,128]{3,2,1,0:T(2,128)} %get-tuple-element.33), channel_id=1, source_target_pairs={{1,0},{2,1},{3,2},{4,3},{5,4},{6,5},{7,6},{9,8},{10,9},{11,10},{12... | collective-permute-start | bytes 147464 | tf_op jit(solution)/shard_map/ppermute | solution.py:34
  21.6 1.7 fusion.256
  23.3 1.9 collective-permute-start.6
  25.3 5.0 %sort.17 = (s32[1152]{0:T(1024)}, s32[1152]{0:T(1024)S(1)}) sort(s32[1152]{0:T(1024)S(1)} %get-tuple-element.65, s32[1152]{0:T(1024)S(1)} %iota.43), dimensions={0}, to_apply=%region_0.1 | sort | flops 12672 | bytes 18432 | tf_op jit(solution)/shard_map/jit(argsort)/sort | solution.py:182
  30.3 0.5 fusion.258
  30.8 0.7 gather_fusion.3
  31.5 0.2 copy.21
  31.7 0.6 gather_fusion.1
  32.3 0.2 slice_reduce_fusion.3
  32.5 0.2 copy.22
  32.8 0.6 gather_fusion.2
  33.3 0.2 slice_reduce_fusion.2
  33.5 2.1 %convolution_bitcast_fusion = f32[3072,9]{0,1:T(8,128)} fusion(f32[3072,128]{1,0:T(8,128)S(1)} %bitcast.54, f32[9]{0:T(128)S(1)} %get-tuple-element.14, s32[9]{0:T(128)S(1)} %get-tuple-element.11), kind=kOutput, calls=%fused_computation.18 | convolution fusion | flops 42490368 | bytes 1683528 | tf_op jit(solution)/shard_map/dot_general | solution.py:195
  35.6 1.1 reshape.177
  36.8 0.7 gather_fusion
  37.5 0.1 fusion.239
  37.6 0.1 copy.27
  37.6 0.7 fusion.233
  38.3 1.2 fusion.230
  39.6 0.2 fusion.173
  39.8 0.9 convolution_bitcast_fusion.1
  40.7 30.1 %all-gather.5 = f32[8,3,1152]{2,1,0:T(4,128)S(1)} all-gather(f32[1,3,1152]{2,1,0:T(4,128)S(1)} %convolution_bitcast_fusion.1), channel_id=2, replica_groups=mesh['gy_0'=8,'gy_1'=4,'gy_2'=2,'gz_0'=2,'gz_1'=4] {'gy_0'}, dimensions={0}, use_global_device_ids=true | all-gather | bytes 124416 | tf_op jit(solution)/shard_map/all_gather | solution.py:21
  70.8 13.2 %all-gather.6 = f32[4,3,1152]{2,1,0:T(4,128)S(1)} all-gather(f32[1,3,1152]{2,1,0:T(4,128)S(1)} %bitcast.61), channel_id=3, replica_groups=mesh['gy_0'=8,'gy_1'=4,'gy_2'=2,'gz_0'=2,'gz_1'=4] {'gy_1'}, dimensions={0}, use_global_device_ids=true | all-gather | bytes 69120 | tf_op jit(solution)/shard_map/all_gather | solution.py:21
  83.9 1.8 all-gather.7
  85.8 8.3 %all-gather.8 = f32[2,3,1152]{2,1,0:T(4,128)S(1)} all-gather(f32[1,3,1152]{2,1,0:T(4,128)S(1)} %bitcast.58), channel_id=5, replica_groups=mesh['gy_0'=8,'gy_1'=4,'gy_2'=2,'gz_0'=2,'gz_1'=4] {'gz_0'}, dimensions={0}, use_global_device_ids=true | all-gather | bytes 41472 | tf_op jit(solution)/shard_map/all_gather | solution.py:21
  94.1 11.9 %all-gather.9 = f32[4,3,1152]{2,1,0:T(4,128)S(1)} all-gather(f32[1,3,1152]{2,1,0:T(4,128)S(1)} %bitcast.60), channel_id=6, replica_groups=mesh['gy_0'=8,'gy_1'=4,'gy_2'=2,'gz_0'=2,'gz_1'=4] {'gz_1'}, dimensions={0}, use_global_device_ids=true | all-gather | bytes 69120 | tf_op jit(solution)/shard_map/all_gather | solution.py:21
  106.8 0.1 add_multiply_fusion
  107.2 1.2 multiply_bitcast_fusion.2
  108.4 1.2 fusion.96
  109.7 0.2 rsqrt_multiply_fusion
  109.9 2.6 %fusion.85 = (f32[16,64,128]{2,1,0:T(8,128)}, f32[16,64,128]{2,1,0:T(8,128)}, f32[16,64,128]{2,1,0:T(8,128)}, f32[16,64,128]{2,1,0:T(8,128)}) fusion(f32[16,64,128]{2,1,0:T(8,128)S(1)} %get-tuple-element.22), kind=kLoop, calls=%fused_computation.192 | loop fusion | flops 9437184 | bytes 2621440 | tf_op jit(solution)/shard_map/jit(_where)/select_n | solution.py:62
  112.5 1.1 copy.23
  113.6 1.6 gather_fusion.4
  115.2 0.1 copy.24
  115.3 9.9 %collective-permute-start.7 = (f32[3,16,2,128]{3,2,1,0:T(2,128)S(1)}, f32[3,16,2,128]{3,2,1,0:T(2,128)S(1)}, u32[]{:S(2)}, u32[]{:S(2)}) collective-permute-start(f32[3,16,2,128]{3,2,1,0:T(2,128)S(1)} %copy-done.7), channel_id=1, source_target_pairs={{1,0},{2,1},{3,2},{4,3},{5,4},{6,5},{7,6},{9,8},{10,9},{11,10},{12... | collective-permute-start | bytes 147464 | tf_op jit(solution)/shard_map/ppermute | solution.py:34
  125.3 0.8 pad.29
  126.1 1.9 collective-permute-start.2
  128.1 6.3 %collective-permute-start.5 = (f32[3,2,64,128]{3,2,1,0:T(8,128)}, f32[3,2,64,128]{3,2,1,0:T(8,128)S(1)}, u32[]{:S(2)}, u32[]{:S(2)}) collective-permute-start(f32[3,2,64,128]{3,2,1,0:T(8,128)} %get-tuple-element.38), channel_id=1, source_target_pairs={{8,0},{16,8},{24,16},{32,24},{40,32},{48,40},{56,48},{64,56},{72,6... | collective-permute-start | bytes 589832 | tf_op jit(solution)/shard_map/ppermute | solution.py:34
  134.4 1.0 constant_dynamic-update-slice_fusion.4
  135.4 1.0 constant_dynamic-update-slice_fusion.8
  136.3 1.2 constant_dynamic-update-slice_fusion.3
  137.6 0.3 pad_maximum_fusion
  138.0 1.0 copy-done.5
  139.1 3.7 %select_maximum_fusion = f32[3,20,68,132]{3,2,1,0:T(8,128)} fusion(f32[3,20,2,128]{3,2,1,0:T(2,128)S(1)} %pad.34, f32[3,20,64,128]{3,2,1,0:T(8,128)S(1)} %get-tuple-element.61, f32[3,20,2,128]{3,2,1,0:T(2,128)S(1)} %pad.33), kind=kLoop, calls=%fused_computation.15 | loop fusion | flops 4308480 | bytes 4243200 | tf_op jit(solution)/shard_map/concatenate | solution.py:40
  142.9 19.1 %fusion.27 = f32[3,16,64,128]{3,2,1,0:T(8,128)} fusion(f32[3,16,64,128]{3,2,1,0:T(8,128)S(1)} %copy-done.1, f32[3,20,64,128]{3,2,1,0:T(8,128)} %copy-done.3, f32[3,20,2,128]{3,2,1,0:T(2,128)S(1)} %pad.34, f32[3,20,2,128]{3,2,1,0:T(2,128)S(1)} %pad.33, f32[3,20,64,128]{3,2,1,0:T(8,128)} %copy-done.2, f32[3,20,2,128]{3,2,1,0:T(2,128)S(1)} %pad.30, ...), kind=kOutput, calls=%fused_computation.67 | convolution fusion | flops 64931328 | bytes 29863944 | tf_op jit(solution)/shard_map/dot_general | solution.py:210
  162.0 6.4 %fusion.45 = f32[3,16,64,128]{3,2,1,0:T(8,128)S(1)} fusion(f32[3,16,64,128]{3,2,1,0:T(8,128)} %fusion.27, f32[16,64,128]{2,1,0:T(8,128)} %get-tuple-element.53, f32[16,64,128]{2,1,0:T(8,128)} %get-tuple-element.52, f32[16,64,128]{2,1,0:T(8,128)} %get-tuple-element.21, f32[16,64,128]{2,1,0:T(8,128)} %get-tuple-element.51, f32[16,64,128]{2,1,0:T(8,128)} %get-tuple-element.50), kind=kLoop, calls=%fused_computation.85 | loop fusion | flops 3538944 | bytes 5767168 | tf_op jit(solution)/shard_map/add | solution.py:103
  168.4 4.8 %collective-permute-start.8 = (f32[3,2,64,128]{3,2,1,0:T(8,128)S(1)}, f32[3,2,64,128]{3,2,1,0:T(8,128)S(1)}, u32[]{:S(2)}, u32[]{:S(2)}) collective-permute-start(f32[3,2,64,128]{3,2,1,0:T(8,128)S(1)} %get-tuple-element.19), channel_id=1, source_target_pairs={{8,0},{16,8},{24,16},{32,24},{40,32},{48,40},{56,48},{64,56},{72,6... | collective-permute-start | bytes 589832 | tf_op jit(solution)/shard_map/ppermute | solution.py:53
  173.2 1.9 collective-permute-start.9
  175.2 0.1 fusion.70
  175.2 1.5 fusion.80
  176.9 0.5 collective-permute-done.8
  177.4 5.6 %collective-permute-done.9 = f32[3,2,64,128]{3,2,1,0:T(8,128)S(1)} collective-permute-done((f32[3,2,64,128]{3,2,1,0:T(8,128)S(1)}, f32[3,2,64,128]{3,2,1,0:T(8,128)S(1)}, u32[]{:S(2)}, u32[]{:S(2)}) %collective-permute-start.9) | collective-permute-done | bytes 196640 | tf_op jit(solution)/shard_map/ppermute | solution.py:52
  182.9 1.3 fusion.12
  184.3 1.9 collective-permute-start.10
  186.2 3.9 %collective-permute-start.11 = (f32[3,16,2,128]{3,2,1,0:T(2,128)S(1)}, f32[3,16,2,128]{3,2,1,0:T(2,128)S(1)}, u32[]{:S(2)}, u32[]{:S(2)}) collective-permute-start(f32[3,16,2,128]{3,2,1,0:T(2,128)S(1)} %get-tuple-element.18), channel_id=1, source_target_pairs={{0,1},{1,2},{2,3},{3,4},{4,5},{5,6},{6,7},{8,9},{9,10},{10,11},{11... | collective-permute-start | bytes 147464 | tf_op jit(solution)/shard_map/ppermute | solution.py:52
  190.2 1.7 fusion.75
  191.8 6.4 %collective-permute-done.11 = f32[3,16,2,128]{3,2,1,0:T(2,128)S(1)} collective-permute-done((f32[3,16,2,128]{3,2,1,0:T(2,128)S(1)}, f32[3,16,2,128]{3,2,1,0:T(2,128)S(1)}, u32[]{:S(2)}, u32[]{:S(2)}) %collective-permute-start.11) | collective-permute-done | bytes 49184 | tf_op jit(solution)/shard_map/ppermute | solution.py:52
  198.2 2.1 %fusion.4 = f32[3,16,64,128]{3,2,1,0:T(8,128)} fusion(f32[3,16,2,128]{3,2,1,0:T(2,128)S(1)} %collective-permute-done.11, f32[3,16,64,128]{3,2,1,0:T(8,128)S(1)} %fusion.12, f32[3,16,2,128]{3,2,1,0:T(2,128)S(1)} %collective-permute-done.10, f32[16,64,128]{2,1,0:T(8,128)S(1)} %get-tuple-element.46, f32[16,64,128]{2,1,0:T(8,128)S(1)} %get-tuple-element.47, ...), kind=kLoop, calls=%fused_computation.44 | loop fusion | flops 5111808 | bytes 5865472 | tf_op jit(solution)/shard_map/add | solution.py:103
  (75 shorter events, 1.0 us)
Async XLA Ops:
  0.6 8.4 %copy-start = (f32[3,16,64,128]{3,2,1,0:T(8,128)S(1)}, f32[3,16,64,128]{3,2,1,0:T(8,128)}, u32[]{:S(2)}) copy-start(f32[3,16,64,128]{3,2,1,0:T(8,128)} %param.9) | copy-start | bytes 4718596
  0.6 24.6 %copy-start.15 = (s32[1152]{0:T(1024)S(1)}, s32[1152]{0:T(1024)}, u32[]{:S(2)}) copy-start(s32[1152]{0:T(1024)} %param.10) | copy-start | bytes 13828
  0.7 30.8 %copy-start.10 = (s32[3,1152]{1,0:T(4,128)S(1)}, s32[3,1152]{1,0:T(4,128)}, u32[]{:S(2)}) copy-start(s32[3,1152]{1,0:T(4,128)} %param.11) | copy-start | bytes 41476
  0.7 31.8 %copy-start.11 = (f32[3,1152]{1,0:T(4,128)S(1)}, f32[3,1152]{1,0:T(4,128)}, u32[]{:S(2)}) copy-start(f32[3,1152]{1,0:T(4,128)} %param.12) | copy-start | bytes 41476
  2.6 131.8 %collective-permute-start.1 = (f32[3,2,64,128]{3,2,1,0:T(8,128)}, f32[3,2,64,128]{3,2,1,0:T(8,128)}, u32[]{:S(2)}, u32[]{:S(2)}) collective-permute-start(f32[3,2,64,128]{3,2,1,0:T(8,128)} %get-tuple-element.35), channel_id=1, source_target_pairs={{0,8},{8,16},{16,24},{24,32},{32,40},{40,48},{48,56},{56,64},{64,7... | collective-permute-start | bytes 589832 | tf_op jit(solution)/shard_map/ppermute | solution.py:33
  6.3 129.0 %collective-permute-start.4 = (f32[3,2,64,128]{3,2,1,0:T(8,128)}, f32[3,2,64,128]{3,2,1,0:T(8,128)}, u32[]{:S(2)}, u32[]{:S(2)}) collective-permute-start(f32[3,2,64,128]{3,2,1,0:T(8,128)} %get-tuple-element.39), channel_id=1, source_target_pairs={{0,8},{8,16},{16,24},{24,32},{32,40},{40,48},{48,56},{56,64},{64,7... | collective-permute-start | bytes 589832 | tf_op jit(solution)/shard_map/ppermute | solution.py:33
  9.7 105.6 %collective-permute-start = (f32[3,16,2,128]{3,2,1,0:T(2,128)}, f32[3,16,2,128]{3,2,1,0:T(2,128)}, u32[]{:S(2)}, u32[]{:S(2)}) collective-permute-start(f32[3,16,2,128]{3,2,1,0:T(2,128)} %get-tuple-element.32), channel_id=1, source_target_pairs={{0,1},{1,2},{2,3},{3,4},{4,5},{5,6},{6,7},{8,9},{9,10},{10,11},{11... | collective-permute-start | bytes 147464 | tf_op jit(solution)/shard_map/ppermute | solution.py:33
  13.1 113.0 %collective-permute-start.3 = (f32[3,16,2,128]{3,2,1,0:T(2,128)}, f32[3,16,2,128]{3,2,1,0:T(2,128)S(1)}, u32[]{:S(2)}, u32[]{:S(2)}) collective-permute-start(f32[3,16,2,128]{3,2,1,0:T(2,128)} %get-tuple-element.33), channel_id=1, source_target_pairs={{1,0},{2,1},{3,2},{4,3},{5,4},{6,5},{7,6},{9,8},{10,9},{11,10},{12... | collective-permute-start | bytes 147464 | tf_op jit(solution)/shard_map/ppermute | solution.py:34
  23.3 104.8 %collective-permute-start.6 = (f32[3,16,2,128]{3,2,1,0:T(2,128)}, f32[3,16,2,128]{3,2,1,0:T(2,128)S(1)}, u32[]{:S(2)}, u32[]{:S(2)}) collective-permute-start(f32[3,16,2,128]{3,2,1,0:T(2,128)} %get-tuple-element.36), channel_id=1, source_target_pairs={{0,1},{1,2},{2,3},{3,4},{4,5},{5,6},{6,7},{8,9},{9,10},{10,11},{11... | collective-permute-start | bytes 147464 | tf_op jit(solution)/shard_map/ppermute | solution.py:33
  33.5 4.0 %copy-start.16 = (f32[9]{0:T(128)}, f32[9]{0:T(128)S(1)}, u32[]{:S(2)}) copy-start(f32[9]{0:T(128)S(1)} %get-tuple-element.14) | copy-start | bytes 112
  35.6 71.1 %copy-start.12 = (f32[1152]{0:T(1024)S(1)}, f32[1152]{0:T(1024)}, u32[]{:S(2)}) copy-start(f32[1152]{0:T(1024)} %param.14) | copy-start | bytes 13828
  35.6 71.1 %copy-start.13 = (f32[1152]{0:T(1024)S(1)}, f32[1152]{0:T(1024)}, u32[]{:S(2)}) copy-start(f32[1152]{0:T(1024)} %param.13) | copy-start | bytes 13828
  35.6 71.5 %copy-start.1 = (f32[3,16,64,128]{3,2,1,0:T(8,128)S(1)}, f32[3,16,64,128]{3,2,1,0:T(8,128)}, u32[]{:S(2)}) copy-start(f32[3,16,64,128]{3,2,1,0:T(8,128)} %param.8) | copy-start | bytes 4718596
  109.9 5.4 %copy-start.7 = (f32[3,16,2,128]{3,2,1,0:T(2,128)S(1)}, f32[3,16,2,128]{3,2,1,0:T(2,128)}, u32[]{:S(2)}) copy-start(f32[3,16,2,128]{3,2,1,0:T(2,128)} %get-tuple-element.37) | copy-start | bytes 147460
  112.5 25.0 %copy-start.6 = (f32[3,1152]{1,0:T(4,128)}, f32[3,1152]{1,0:T(4,128)S(1)}, u32[]{:S(2)}) copy-start(f32[3,1152]{1,0:T(4,128)S(1)} %pad_maximum_fusion.9) | copy-start | bytes 41476
  115.3 19.0 %collective-permute-start.7 = (f32[3,16,2,128]{3,2,1,0:T(2,128)S(1)}, f32[3,16,2,128]{3,2,1,0:T(2,128)S(1)}, u32[]{:S(2)}, u32[]{:S(2)}) collective-permute-start(f32[3,16,2,128]{3,2,1,0:T(2,128)S(1)} %copy-done.7), channel_id=1, source_target_pairs={{1,0},{2,1},{3,2},{4,3},{5,4},{6,5},{7,6},{9,8},{10,9},{11,10},{12... | collective-permute-start | bytes 147464 | tf_op jit(solution)/shard_map/ppermute | solution.py:34
  126.1 11.5 %collective-permute-start.2 = (f32[3,2,64,128]{3,2,1,0:T(8,128)}, f32[3,2,64,128]{3,2,1,0:T(8,128)S(1)}, u32[]{:S(2)}, u32[]{:S(2)}) collective-permute-start(f32[3,2,64,128]{3,2,1,0:T(8,128)} %get-tuple-element.34), channel_id=1, source_target_pairs={{8,0},{16,8},{24,16},{32,24},{40,32},{48,40},{56,48},{64,56},{72,6... | collective-permute-start | bytes 589832 | tf_op jit(solution)/shard_map/ppermute | solution.py:34
  128.1 11.0 %collective-permute-start.5 = (f32[3,2,64,128]{3,2,1,0:T(8,128)}, f32[3,2,64,128]{3,2,1,0:T(8,128)S(1)}, u32[]{:S(2)}, u32[]{:S(2)}) collective-permute-start(f32[3,2,64,128]{3,2,1,0:T(8,128)} %get-tuple-element.38), channel_id=1, source_target_pairs={{8,0},{16,8},{24,16},{32,24},{40,32},{48,40},{56,48},{64,56},{72,6... | collective-permute-start | bytes 589832 | tf_op jit(solution)/shard_map/ppermute | solution.py:34
  137.5 5.3 %copy-start.8 = (f32[3,18,64,128]{3,2,1,0:T(8,128)}, f32[3,18,64,128]{3,2,1,0:T(8,128)S(1)}, u32[]{:S(2)}) copy-start(f32[3,18,64,128]{3,2,1,0:T(8,128)S(1)} %get-tuple-element.26) | copy-start | bytes 5308420
  137.6 5.3 %copy-start.9 = (f32[3,18,64,128]{3,2,1,0:T(8,128)}, f32[3,18,64,128]{3,2,1,0:T(8,128)S(1)}, u32[]{:S(2)}) copy-start(f32[3,18,64,128]{3,2,1,0:T(8,128)S(1)} %get-tuple-element.75) | copy-start | bytes 5308420
  137.6 1.4 copy-start.5
  137.6 5.2 %copy-start.2 = (f32[3,20,64,128]{3,2,1,0:T(8,128)}, f32[3,20,64,128]{3,2,1,0:T(8,128)S(1)}, u32[]{:S(2)}) copy-start(f32[3,20,64,128]{3,2,1,0:T(8,128)S(1)} %get-tuple-element.57) | copy-start | bytes 5898244
  139.1 3.8 %copy-start.4 = (f32[3,18,64,128]{3,2,1,0:T(8,128)}, f32[3,18,64,128]{3,2,1,0:T(8,128)S(1)}, u32[]{:S(2)}) copy-start(f32[3,18,64,128]{3,2,1,0:T(8,128)S(1)} %get-tuple-element.60) | copy-start | bytes 5308420
  139.1 3.8 %copy-start.3 = (f32[3,20,64,128]{3,2,1,0:T(8,128)}, f32[3,20,64,128]{3,2,1,0:T(8,128)S(1)}, u32[]{:S(2)}) copy-start(f32[3,20,64,128]{3,2,1,0:T(8,128)S(1)} %get-tuple-element.61) | copy-start | bytes 5898244
  139.1 3.8 %copy-start.14 = (f32[9,64]{1,0:T(8,128)S(1)}, f32[9,64]{1,0:T(8,128)}, u32[]{:S(2)}) copy-start(f32[9,64]{1,0:T(8,128)} %get-tuple-element.72) | copy-start | bytes 6916
  139.1 3.8 %copy-start.17 = (f32[9]{0:T(128)S(1)}, f32[9]{0:T(128)}, u32[]{:S(2)}) copy-start(f32[9]{0:T(128)} %copy-done.16) | copy-start | bytes 112
  168.4 8.9 %collective-permute-start.8 = (f32[3,2,64,128]{3,2,1,0:T(8,128)S(1)}, f32[3,2,64,128]{3,2,1,0:T(8,128)S(1)}, u32[]{:S(2)}, u32[]{:S(2)}) collective-permute-start(f32[3,2,64,128]{3,2,1,0:T(8,128)S(1)} %get-tuple-element.19), channel_id=1, source_target_pairs={{8,0},{16,8},{24,16},{32,24},{40,32},{48,40},{56,48},{64,56},{72,6... | collective-permute-start | bytes 589832 | tf_op jit(solution)/shard_map/ppermute | solution.py:53
  173.2 9.7 %collective-permute-start.9 = (f32[3,2,64,128]{3,2,1,0:T(8,128)S(1)}, f32[3,2,64,128]{3,2,1,0:T(8,128)S(1)}, u32[]{:S(2)}, u32[]{:S(2)}) collective-permute-start(f32[3,2,64,128]{3,2,1,0:T(8,128)S(1)} %get-tuple-element.20), channel_id=1, source_target_pairs={{0,8},{8,16},{16,24},{24,32},{32,40},{40,48},{48,56},{56,64},{64,7... | collective-permute-start | bytes 589832 | tf_op jit(solution)/shard_map/ppermute | solution.py:52
  184.3 7.5 %collective-permute-start.10 = (f32[3,16,2,128]{3,2,1,0:T(2,128)S(1)}, f32[3,16,2,128]{3,2,1,0:T(2,128)S(1)}, u32[]{:S(2)}, u32[]{:S(2)}) collective-permute-start(f32[3,16,2,128]{3,2,1,0:T(2,128)S(1)} %get-tuple-element.17), channel_id=1, source_target_pairs={{1,0},{2,1},{3,2},{4,3},{5,4},{6,5},{7,6},{9,8},{10,9},{11,10},{12... | collective-permute-start | bytes 147464 | tf_op jit(solution)/shard_map/ppermute | solution.py:53
  186.2 12.0 %collective-permute-start.11 = (f32[3,16,2,128]{3,2,1,0:T(2,128)S(1)}, f32[3,16,2,128]{3,2,1,0:T(2,128)S(1)}, u32[]{:S(2)}, u32[]{:S(2)}) collective-permute-start(f32[3,16,2,128]{3,2,1,0:T(2,128)S(1)} %get-tuple-element.18), channel_id=1, source_target_pairs={{0,1},{1,2},{2,3},{3,4},{4,5},{5,6},{6,7},{8,9},{9,10},{10,11},{11... | collective-permute-start | bytes 147464 | tf_op jit(solution)/shard_map/ppermute | solution.py:52
